TPU v7x, 32 devices: a whole 2x2x4 slice. The times are simulated.
32 devices in a mesh: dp: 8 (over z, y), tensor: 4 (over x, core).
Axes of the slice: x: 2, y: 2, z: 4, core: 2. Of those that a mesh axis runs over, the one named last changes fastest.
Arguments:
- logits: bfloat16 [32, 64, 152064], P('dp', None, 'tensor'), may hold values from -3 to 3
- tokens: int32 [32, 64], P('dp'), may hold values from 0 to 152063
- lengths: int32 [32], P('dp'), may hold values from 1 to 64, 1024 in all
- group_ids: int32 [32], P('dp'), may hold values from 0 to 1, as said below
- rewards: float32 [32], P('dp'), may hold values from -4 to 4
- old_logp: float32 [32, 64], P('dp'), may hold values from -12.6 to -11.5
- ref_logp: float32 [32, 64], P('dp'), may hold values from -12.6 to -11.5
Outputs:
- token_logp: float32 [32, 64], P('dp')
- advantages: float32 [32], P('dp')
- seq_loss: float32 [32], P('dp')
- total_loss: float32 [], replicated
Inputs may be any that keep to these rules, and one draw needn't show every extreme that they name: `group_ids`: each number 0 to 1 names exactly 16 responses, placed at random over the batch. `lengths`: each response has 1 to 64 tokens, the longest exactly 64.
All inputs are finite; a program needn't handle non-finite values.
Results may differ from a plain program's by a relative error of at most 0.0003.
Values sent between devices are 32-bit elements.
A program may use at most 128 MiB of HBM per device.

v0:
```python
import jax
import jax.numpy as jnp
from jax import lax
from jax.sharding import PartitionSpec as P

GROUP = 16
CLIP_LOW = 0.2
CLIP_HIGH = 0.28
KL_WEIGHT = 0.04
STD_EPS = 0.0001


def combined_all(value, axis, join):
    pieces = jax.tree.map(lambda part: lax.all_gather(part, axis), value)
    head = jax.tree.map(lambda part: part[0], pieces)
    tail = jax.tree.map(lambda part: part[1:], pieces)
    total, _ = lax.scan(lambda total, slab: (join(total, slab), None), head, tail)
    return total


def combine_pair(former, latter):
    row_peak = jnp.maximum(former[0], latter[0])
    row_total = former[1] * jnp.exp(former[0] - row_peak) + latter[1] * jnp.exp(
        latter[0] - row_peak
    )
    return (row_peak, row_total)


def block_stats(logit_block, local_ids, vocab_width):
    values = logit_block.astype(jnp.float32)
    row_peak = jnp.max(values, axis=-1)
    row_total = jnp.sum(jnp.exp(values - row_peak[..., None]), axis=-1)
    inside = (local_ids >= 0) & (local_ids < vocab_width)
    clamped = jnp.clip(local_ids, 0, vocab_width - 1)
    picked = jnp.take_along_axis(values, clamped[..., None], axis=-1)[..., 0]
    return (row_peak, row_total, jnp.where(inside, picked, 0.0))


def local(logits, tokens, lengths, group_ids, rewards, old_logp, ref_logp):
    resp_count, seq_len, vocab_width = logits.shape
    vocab_start = lax.axis_index("tensor") * vocab_width
    local_ids = tokens - vocab_start
    positions = lax.broadcasted_iota(jnp.int32, (resp_count, seq_len), 1)
    is_valid = positions < lengths[:, None]
    row_peak, row_total, picked = block_stats(logits, local_ids, vocab_width)
    row_peak, row_total = combined_all((row_peak, row_total), "tensor", combine_pair)
    picked = lax.psum(picked, "tensor")
    token_logp = jnp.where(is_valid, picked - row_peak - jnp.log(row_total), 0.0)
    group_count = resp_count * lax.axis_size("dp") // GROUP
    group_sum, squares = lax.psum(
        (
            jax.ops.segment_sum(rewards, group_ids, num_segments=group_count),
            jax.ops.segment_sum(rewards * rewards, group_ids, num_segments=group_count),
        ),
        "dp",
    )
    group_mean = group_sum / GROUP
    spread = rewards - group_mean[group_ids]
    deviation = jnp.sqrt(jnp.maximum(squares - group_sum * group_mean, 0.0) / (GROUP - 1))
    advantages = spread / (deviation[group_ids] + STD_EPS)
    prob_ratio = jnp.exp(token_logp - old_logp)
    clipped = jnp.clip(prob_ratio, 1.0 - CLIP_LOW, 1.0 + CLIP_HIGH)
    token_gain = advantages[:, None]
    policy = -jnp.minimum(prob_ratio * token_gain, clipped * token_gain)
    ref_drift = ref_logp - token_logp
    penalty = jnp.exp(ref_drift) - ref_drift - 1.0
    token_terms = jnp.where(is_valid, policy + KL_WEIGHT * penalty, 0.0)
    seq_loss = jnp.sum(token_terms, axis=1) / lengths.astype(jnp.float32)
    total_loss = lax.psum(jnp.sum(seq_loss), "dp") / (resp_count * lax.axis_size("dp"))
    return (token_logp, advantages, seq_loss, total_loss)


def solution(mesh):
    in_specs = (
        P("dp", None, "tensor"),
        P("dp", None),
        P("dp"),
        P("dp"),
        P("dp"),
        P("dp", None),
        P("dp", None),
    )
    out_specs = (P("dp", None), P("dp"), P("dp"), P())
    return jax.shard_map(local, mesh=mesh, in_specs=in_specs, out_specs=out_specs, check_vma=False)
```

profile of v0, /device:TPU:0, one launch (start us, length us, event | category | flops | bytes accessed | tf_op | source)
XLA Modules:
  0.0 109.3 jit_solution(2576854799696201980)
XLA Ops:
  0.6 0.0 copy-start
  0.6 0.7 compare_select_fusion.1
  1.3 0.7 scatter_custom_fusion
  2.0 0.7 mul.36
  2.8 0.7 scatter_custom_fusion.1
  3.5 23.2 %all-reduce = (f32[2]{0:T(128)S(1)}, f32[2]{0:T(128)S(1)}) all-reduce(f32[2]{0:T(128)S(1)} %scatter_custom_fusion.1, f32[2]{0:T(128)S(1)} %scatter_custom_fusion), channel_id=1, replica_groups=mesh['dp'=8,'tensor'=4] {'dp'}, use_global_device_ids=true, to_apply=%region_8.9 | all-reduce | flops 4 | bytes 32 | tf_op jit(solution)/shard_map/psum | solution.py:50
  26.7 0.7 fusion.12
  27.4 0.1 reshape.64
  27.5 0.6 gather_fusion.1
  28.1 0.6 gather_fusion
  28.8 0.7 add_divide_fusion
  29.4 0.0 copy-start.2
  29.4 0.0 copy-start.1
  29.4 0.0 copy-start.3
  29.4 0.0 copy-start.4
  29.4 28.6 %fusion.18 = (f32[4,64,38016]{2,1,0:T(8,128)}, bf16[4,64]{1,0:T(4,128)(2,1)S(1)}) fusion(bf16[4,64,38016]{2,1,0:T(8,128)(2,1)} %param.9), kind=kLoop, calls=%fused_computation.45 | loop fusion | flops 19463936 | bytes 58393088 | tf_op jit(solution)/shard_map/convert_element_type | solution.py:30
  58.0 4.2 %gather_fusion.2 = f32[256]{0:T(256)S(1)} fusion(f32[4,64,38016]{2,1,0:T(8,128)} %get-tuple-element.52, s32[256]{0:T(256)S(1)} %reshape.64), kind=kCustom, calls=%fused_computation.2 | custom fusion | bytes 5120 | tf_op jit(solution)/shard_map/jit(take_along_axis)/gather | solution.py:35
  62.2 0.1 gather.13
  62.3 0.0 copy-done
  62.3 5.7 %psum.28 = f32[4,64]{1,0:T(4,128)S(1)} all-reduce(f32[4,64]{1,0:T(4,128)S(1)} %select_select_fusion), channel_id=1, replica_groups=mesh['dp'=8,'tensor'=4] {'tensor'}, use_global_device_ids=true, to_apply=%region_0.0 | all-reduce | flops 256 | bytes 2048 | tf_op jit(solution)/shard_map/psum | solution.py:47
  68.0 9.4 %exponential_reduce_fusion = f32[4,64]{1,0:T(4,128)S(1)} fusion(f32[4,64]{1,0:T(4,128)S(1)} %get-tuple-element.54, bf16[4,64,38016]{2,1,0:T(8,128)(2,1)} %param.9), kind=kLoop, calls=%fused_computation.10 | loop fusion | flops 29196032 | bytes 19466240 | tf_op jit(solution)/shard_map/reduce_sum | solution.py:32
  77.4 5.2 %all-gather.3 = f32[4,4,64]{2,1,0:T(4,128)S(1)} all-gather(f32[1,4,64]{2,1,0:T(4,128)S(1)} %bitcast.27), channel_id=3, replica_groups=mesh['dp'=8,'tensor'=4] {'tensor'}, dimensions={0}, use_global_device_ids=true | all-gather | bytes 5120 | tf_op jit(solution)/shard_map/all_gather | solution.py:14
  82.6 5.2 %all-gather.2 = f32[4,4,64]{2,1,0:T(4,128)S(1)} all-gather(f32[1,4,64]{2,1,0:T(4,128)S(1)} %get-tuple-element.55), channel_id=2, replica_groups=mesh['dp'=8,'tensor'=4] {'tensor'}, dimensions={0}, use_global_device_ids=true | all-gather | bytes 5120 | tf_op jit(solution)/shard_map/all_gather | solution.py:14
  87.8 0.1 while.12
  87.9 0.0 copy-done.2
  87.9 0.0 copy-done.1
  87.9 0.0 copy-done.3
  87.9 0.0 copy-done.4
  87.9 0.8 fusion.11
  88.7 1.1 %fusion.17 = (f32[]{:T(128)}, f32[4]{0:T(128)}) fusion(f32[4]{0:T(128)S(1)} %get-tuple-element.50, s32[4]{0:T(128)S(1)} %copy-done.1), kind=kLoop, calls=%fused_computation.44 | loop fusion | flops 11 | bytes 52 | tf_op jit(solution)/shard_map/reduce_sum | solution.py:69
  89.8 17.7 %psum.31 = f32[]{:T(128)} all-reduce(f32[]{:T(128)} %get-tuple-element.48), channel_id=1, replica_groups=mesh['dp'=8,'tensor'=4] {'dp'}, use_global_device_ids=true, to_apply=%region_11.12 | all-reduce | flops 1 | bytes 8 | tf_op jit(solution)/shard_map/psum | solution.py:69
  (15 shorter events, 0.1 us)
Async XLA Ops:
  0.6 61.7 %copy-start = (s32[4,64]{1,0:T(4,128)S(1)}, s32[4,64]{1,0:T(4,128)}, u32[]{:S(2)}) copy-start(s32[4,64]{1,0:T(4,128)} %param.10) | copy-start | bytes 3076
  29.4 58.5 %copy-start.2 = (f32[4]{0:T(128)}, f32[4]{0:T(128)S(1)}, u32[]{:S(2)}) copy-start(f32[4]{0:T(128)S(1)} %add_divide_fusion) | copy-start | bytes 52
  29.4 58.5 %copy-start.1 = (s32[4]{0:T(128)S(1)}, s32[4]{0:T(128)}, u32[]{:S(2)}) copy-start(s32[4]{0:T(128)} %param.11) | copy-start | bytes 52
  29.4 58.5 %copy-start.3 = (f32[4,64]{1,0:T(4,128)S(1)}, f32[4,64]{1,0:T(4,128)}, u32[]{:S(2)}) copy-start(f32[4,64]{1,0:T(4,128)} %param.15) | copy-start | bytes 3076
  29.4 58.5 %copy-start.4 = (f32[4,64]{1,0:T(4,128)S(1)}, f32[4,64]{1,0:T(4,128)}, u32[]{:S(2)}) copy-start(f32[4,64]{1,0:T(4,128)} %param.14) | copy-start | bytes 3076
where the time goes:
time: 110 us; the launch traced here: 109 us
  blocking collectives  56.9 us (52%)
  other arithmetic  44.2 us (40%)
  local copies, waits for them, and re-layouts  5.64 us (5%)
  between operations  2.52 us (2%)
    convert_element_type x1, other arithmetic, block_stats(): values = logit_block.astype(jnp.float32)  28.6 us
    psum x1, blocking collectives, local(): lax.psum((jax.ops.segment_sum(rewards, group_ids, num_segments=group_coun...  23.2 us
    psum x1, blocking collectives, local(): lax.psum(jnp.sum(seq_loss), 'dp') / (resp_count * lax.axis_size('dp'))  17.7 us
    all_gather x2, blocking collectives, combined_all(): pieces = jax.tree.map(lambda part: lax.all_gather(part, axis), value)  10.4 us
    reduce_sum x1, other arithmetic, block_stats(): row_total = jnp.sum(jnp.exp(values - row_peak[..., None]), axis=-1)  9.42 us
    psum x1, blocking collectives, local(): picked = lax.psum(picked, 'tensor')  5.67 us
    gather x3, local copies, waits for them, and re-layouts, block_stats(): picked = jnp.take_along_axis(values, clamped[..., None], axis=-1)[..., 0]  4.33 us

commit v1 on v0

--- a/solution.py
+++ b/solution.py
@@ -8,6 +8,12 @@
 CLIP_HIGH = 0.28
 KL_WEIGHT = 0.04
 STD_EPS = 0.0001
+
+
+def add_all(x, name):
+    shards = lax.all_gather(x, name, axis=0, tiled=False)
+    result = shards.sum(axis=0)
+    return result
 
 
 def combined_all(value, axis, join):
@@ -44,7 +50,7 @@
     is_valid = positions < lengths[:, None]
     row_peak, row_total, picked = block_stats(logits, local_ids, vocab_width)
     row_peak, row_total = combined_all((row_peak, row_total), "tensor", combine_pair)
-    picked = lax.psum(picked, "tensor")
+    picked = add_all(picked, "tensor")
     token_logp = jnp.where(is_valid, picked - row_peak - jnp.log(row_total), 0.0)
     group_count = resp_count * lax.axis_size("dp") // GROUP
     group_sum, squares = lax.psum(

time: 110 us -> 109 us (level)
    psum x1 -> x0, blocking collectives: 5.67 us -> none  [local(): picked = lax.psum(picked, 'tensor')]
    all_gather x0 -> x1, blocking collectives: none -> 5.18 us  [add_all(): shards = lax.all_gather(x, name, axis=0, tiled=False)]
where the time goes in v1:
time: 109 us
  blocking collectives  56.4 us (52%)
  other arithmetic  44.2 us (41%)
  local copies, waits for them, and re-layouts  5.64 us (5%)
  between operations  2.53 us (2%)
    convert_element_type x1, other arithmetic, block_stats(): values = logit_block.astype(jnp.float32)  28.6 us
    psum x1, blocking collectives, local(): lax.psum((jax.ops.segment_sum(rewards, group_ids, num_segments=group_coun...  23.2 us
    psum x1, blocking collectives, local(): lax.psum(jnp.sum(seq_loss), 'dp') / (resp_count * lax.axis_size('dp'))  17.7 us
    all_gather x2, blocking collectives, combined_all(): pieces = jax.tree.map(lambda part: lax.all_gather(part, axis), value)  10.4 us
    reduce_sum x1, other arithmetic, block_stats(): row_total = jnp.sum(jnp.exp(values - row_peak[..., None]), axis=-1)  9.43 us
    all_gather x1, blocking collectives, add_all(): shards = lax.all_gather(x, name, axis=0, tiled=False)  5.18 us
    gather x3, local copies, waits for them, and re-layouts, block_stats(): picked = jnp.take_along_axis(values, clamped[..., None], axis=-1)[..., 0]  4.33 us

profile of v1, /device:TPU:0, one launch (start us, length us, event | category | flops | bytes accessed | tf_op | source)
XLA Modules:
  0.0 108.9 jit_solution(844881406953367981)
XLA Ops:
  0.6 0.0 copy-start
  0.6 0.7 compare_select_fusion.1
  1.3 0.7 scatter_custom_fusion
  2.0 0.7 mul.36
  2.8 0.7 scatter_custom_fusion.1
  3.5 23.2 %all-reduce = (f32[2]{0:T(128)S(1)}, f32[2]{0:T(128)S(1)}) all-reduce(f32[2]{0:T(128)S(1)} %scatter_custom_fusion.1, f32[2]{0:T(128)S(1)} %scatter_custom_fusion), channel_id=1, replica_groups=mesh['dp'=8,'tensor'=4] {'dp'}, use_global_device_ids=true, to_apply=%region_8.9 | all-reduce | flops 4 | bytes 32 | tf_op jit(solution)/shard_map/psum | solution.py:56
  26.7 0.7 fusion.12
  27.4 0.1 reshape.64
  27.5 0.6 gather_fusion.1
  28.1 0.6 gather_fusion
  28.8 0.7 add_divide_fusion
  29.4 0.0 copy-start.2
  29.4 0.0 copy-start.1
  29.4 0.0 copy-start.3
  29.4 0.0 copy-start.4
  29.4 28.6 %fusion.18 = (f32[4,64,38016]{2,1,0:T(8,128)}, bf16[4,64]{1,0:T(4,128)(2,1)S(1)}) fusion(bf16[4,64,38016]{2,1,0:T(8,128)(2,1)} %param.9), kind=kLoop, calls=%fused_computation.45 | loop fusion | flops 19463936 | bytes 58393088 | tf_op jit(solution)/shard_map/convert_element_type | solution.py:36
  58.0 4.2 %gather_fusion.2 = f32[256]{0:T(256)S(1)} fusion(f32[4,64,38016]{2,1,0:T(8,128)} %get-tuple-element.52, s32[256]{0:T(256)S(1)} %reshape.64), kind=kCustom, calls=%fused_computation.2 | custom fusion | bytes 5120 | tf_op jit(solution)/shard_map/jit(take_along_axis)/gather | solution.py:41
  62.2 0.1 gather.13
  62.3 0.0 copy-done
  62.3 9.4 %exponential_reduce_fusion = f32[4,64]{1,0:T(4,128)S(1)} fusion(f32[4,64]{1,0:T(4,128)S(1)} %get-tuple-element.54, bf16[4,64,38016]{2,1,0:T(8,128)(2,1)} %param.9), kind=kLoop, calls=%fused_computation.10 | loop fusion | flops 29196032 | bytes 19466240 | tf_op jit(solution)/shard_map/reduce_sum | solution.py:38
  71.7 5.2 %all-gather.5 = f32[4,4,64]{2,1,0:T(4,128)S(1)} all-gather(f32[1,4,64]{2,1,0:T(4,128)S(1)} %bitcast.29), channel_id=4, replica_groups=mesh['dp'=8,'tensor'=4] {'tensor'}, dimensions={0}, use_global_device_ids=true | all-gather | bytes 5120 | tf_op jit(solution)/shard_map/all_gather | solution.py:20
  76.9 5.2 %all-gather.3 = f32[4,4,64]{2,1,0:T(4,128)S(1)} all-gather(f32[1,4,64]{2,1,0:T(4,128)S(1)} %select_bitcast_fusion), channel_id=2, replica_groups=mesh['dp'=8,'tensor'=4] {'tensor'}, dimensions={0}, use_global_device_ids=true | all-gather | bytes 5120 | tf_op jit(solution)/shard_map/all_gather | solution.py:14
  82.1 5.2 %all-gather.4 = f32[4,4,64]{2,1,0:T(4,128)S(1)} all-gather(f32[1,4,64]{2,1,0:T(4,128)S(1)} %get-tuple-element.55), channel_id=3, replica_groups=mesh['dp'=8,'tensor'=4] {'tensor'}, dimensions={0}, use_global_device_ids=true | all-gather | bytes 5120 | tf_op jit(solution)/shard_map/all_gather | solution.py:20
  87.3 0.1 while.12
  87.4 0.0 copy-done.2
  87.4 0.0 copy-done.1
  87.4 0.0 copy-done.3
  87.4 0.0 copy-done.4
  87.4 0.8 fusion.11
  88.2 1.1 %fusion.17 = (f32[]{:T(128)}, f32[4]{0:T(128)}) fusion(f32[4]{0:T(128)S(1)} %get-tuple-element.50, s32[4]{0:T(128)S(1)} %copy-done.1), kind=kLoop, calls=%fused_computation.44 | loop fusion | flops 11 | bytes 52 | tf_op jit(solution)/shard_map/reduce_sum | solution.py:75
  89.3 17.7 %psum.23 = f32[]{:T(128)} all-reduce(f32[]{:T(128)} %get-tuple-element.48), channel_id=1, replica_groups=mesh['dp'=8,'tensor'=4] {'dp'}, use_global_device_ids=true, to_apply=%region_11.12 | all-reduce | flops 1 | bytes 8 | tf_op jit(solution)/shard_map/psum | solution.py:75
  (16 shorter events, 0.1 us)
Async XLA Ops:
  0.6 61.7 %copy-start = (s32[4,64]{1,0:T(4,128)S(1)}, s32[4,64]{1,0:T(4,128)}, u32[]{:S(2)}) copy-start(s32[4,64]{1,0:T(4,128)} %param.10) | copy-start | bytes 3076
  29.4 58.0 %copy-start.2 = (f32[4]{0:T(128)}, f32[4]{0:T(128)S(1)}, u32[]{:S(2)}) copy-start(f32[4]{0:T(128)S(1)} %add_divide_fusion) | copy-start | bytes 52
  29.4 58.0 %copy-start.1 = (s32[4]{0:T(128)S(1)}, s32[4]{0:T(128)}, u32[]{:S(2)}) copy-start(s32[4]{0:T(128)} %param.11) | copy-start | bytes 52
  29.4 58.0 %copy-start.3 = (f32[4,64]{1,0:T(4,128)S(1)}, f32[4,64]{1,0:T(4,128)}, u32[]{:S(2)}) copy-start(f32[4,64]{1,0:T(4,128)} %param.15) | copy-start | bytes 3076
  29.4 58.0 %copy-start.4 = (f32[4,64]{1,0:T(4,128)S(1)}, f32[4,64]{1,0:T(4,128)}, u32[]{:S(2)}) copy-start(f32[4,64]{1,0:T(4,128)} %param.14) | copy-start | bytes 3076
